TPU v7x, 32 devices: a whole 2x2x4 slice. The times are simulated.
32 devices in a mesh: vocab: 16 (over z, y, x), pipe: 2 (over core).
Axes of the slice: x: 2, y: 2, z: 4, core: 2. Of those that a mesh axis runs over, the one named last changes fastest.
Arguments:
- hidden_a: bfloat16 [512, 4096], P('pipe', 'vocab'), parts along dimension 0, may hold values from -8 to 8, as said below
- labels_a: int32 [512], P('pipe'), parts along dimension 0, may hold values from 0 to 8191
- hidden_b: bfloat16 [512, 4096], P('pipe', 'vocab'), parts along dimension 0, may hold values from -8 to 8, as said below
- labels_b: int32 [512], P('pipe'), parts along dimension 0, may hold values from 0 to 8191
- loss_cotangent: float32 [512], P('pipe'), parts along dimension 0, may hold values from -192 to 192
- out_weight: bfloat16 [8192, 8192], P('pipe', 'vocab'), parts along dimension 0, may hold values from -0.28125 to 0.28125, as said below
Outputs:
- logits_a: bfloat16 [512, 8192], P('pipe', 'vocab'), parts along dimension 0
- loss_a: float32 [512], P('pipe'), parts along dimension 0
- amax_scale: float32 [2], P('pipe'), parts along dimension 0
- grad_hidden_b: bfloat16 [512, 4096], P('pipe', 'vocab'), parts along dimension 0
There are 2 independent parts, one for each index of `pipe`. A program takes and returns all parts, laid end to end along the dimension named above; each array names one. Nothing has to cross between parts.
Inputs may be any that keep to these rules, and one draw needn't show every extreme that they name: `hidden_a`: hidden states of order one. `hidden_b`: hidden states of order one. `out_weight`: entries of scale 3 over the square root of 4096.
All inputs are finite; a program needn't handle non-finite values. Where the computation divides by a largest or mean magnitude, that divisor is 1e-20 or more.
Results may differ from a plain program's by a relative error of at most 0.0048.
Values may be sent and summed in bfloat16 or wider, within the bound.
A program may use at most 64 MiB of HBM per device.

v0:
```python
import jax
import jax.numpy as jnp
from jax import lax
from jax.sharding import PartitionSpec as P


def shards(hidden_a, labels_a, hidden_b, labels_b, loss_cotangent, out_weight):
    vocab_rows = out_weight.shape[1]
    offset = lax.axis_index("vocab") * vocab_rows

    def accumulate(portion):
        return jnp.dot(portion, out_weight, preferred_element_type=jnp.float32)

    scores_a = accumulate(lax.all_gather(hidden_a, "vocab", axis=1, tiled=True))
    scores_b = accumulate(lax.all_gather(hidden_b, "vocab", axis=1, tiled=True))
    columns_a = offset + lax.broadcasted_iota(jnp.int32, scores_a.shape, 1)
    columns_b = offset + lax.broadcasted_iota(jnp.int32, scores_b.shape, 1)
    label_local = jnp.sum(jnp.where(columns_a == labels_a[:, None], scores_a, 0.0), axis=1)
    row_peak_a = jnp.max(scores_a, axis=1)
    abs_peak = jnp.max(jnp.abs(scores_a)).reshape(1)
    row_peak_b = jnp.max(scores_b, axis=1)
    peak_a, largest = lax.pmax((row_peak_a, abs_peak), "vocab")
    own_total_a = jnp.sum(jnp.exp(scores_a - peak_a[:, None]), axis=1)
    total_a, label_a = lax.psum((own_total_a, label_local), "vocab")
    peak_b = lax.pmax(row_peak_b, "vocab")
    own_total_b = jnp.sum(jnp.exp(scores_b - peak_b[:, None]), axis=1)
    total_b = lax.psum(own_total_b, "vocab")
    loss_a = jnp.log(total_a) + peak_a - label_a
    amax_scale = 448.0 / largest
    onehot = (columns_b == labels_b[:, None]).astype(jnp.float32)
    probs = jnp.exp(scores_b - peak_b[:, None]) / total_b[:, None]
    dlogits_b = ((probs - onehot) * loss_cotangent[:, None]).astype(jnp.bfloat16)
    grad_terms = lax.dot_general(
        dlogits_b, out_weight, (((1,), (1,)), ((), ())), preferred_element_type=jnp.float32
    )
    grad_hidden_b = lax.psum_scatter(grad_terms, "vocab", scatter_dimension=1, tiled=True).astype(
        jnp.bfloat16
    )
    return (scores_a.astype(jnp.bfloat16), loss_a, amax_scale, grad_hidden_b)


def solution(mesh):
    return jax.shard_map(
        shards,
        mesh=mesh,
        in_specs=(
            P("pipe", "vocab"),
            P("pipe"),
            P("pipe", "vocab"),
            P("pipe"),
            P("pipe"),
            P("pipe", "vocab"),
        ),
        out_specs=(P("pipe", "vocab"), P("pipe"), P("pipe"), P("pipe", "vocab")),
        check_vma=False,
    )
```

profile of v0, /device:TPU:0, one launch (start us, length us, event | category | flops | bytes accessed | tf_op | source)
XLA Modules:
  0.0 332.6 jit_solution(5259473569760511634)
XLA Ops:
  7.2 0.0 copy-start.2
  7.2 0.0 all-gather.3.cloned.1.call-start
  7.2 0.7 all-gather.3.cloned.1.call-update
  7.9 0.0 all-gather.5.cloned.1.call-start
  8.0 0.7 all-gather.5.cloned.1.call-update
  8.7 0.0 reduce-scatter.2.cloned.1.call-start
  8.7 69.5 %all-gather.3.cloned.1.call-done = bf16[256,4096]{1,0:T(8,128)(2,1)} async-done(((bf16[256,256]{1,0:T(8,128)(2,1)}), bf16[256,4096]{1,0:T(8,128)(2,1)}) %all-gather.3.cloned.1.call-update) | async-done | bytes 2097168 | tf_op jit(solution)/shard_map/all_gather | solution.py:14
  78.2 4.1 %fusion.7 = (f32[256]{0:T(256)S(1)}, f32[256,512]{1,0:T(8,128)S(1)}) fusion(bf16[256,4096]{1,0:T(8,128)(2,1)} %all-gather.3.cloned.1.call-done, bf16[4096,512]{1,0:T(8,128)(2,1)} %param.11), kind=kOutput, calls=%fused_computation.14 | convolution fusion | flops 1073872640 | bytes 6816768 | tf_op jit(solution)/shard_map/dot_general | solution.py:12
  82.3 38.8 %pmax.21 = f32[256]{0:T(256)S(1)} all-reduce(f32[256]{0:T(256)S(1)} %get-tuple-element.13), channel_id=1, replica_groups=mesh['vocab'=16,'pipe'=2] {'vocab'}, use_global_device_ids=true, to_apply=%region_1.2 | all-reduce | flops 256 | bytes 2048 | tf_op jit(solution)/shard_map/pmax | solution.py:22
  121.1 0.0 copy-done.2
  121.1 1.5 abs_reduce_fusion
  122.7 0.0 copy-start
  122.7 0.0 copy-start.1
  122.7 21.5 %all-gather.5.cloned.1.call-done = bf16[256,4096]{1,0:T(8,128)(2,1)} async-done(((bf16[256,256]{1,0:T(8,128)(2,1)}), bf16[256,4096]{1,0:T(8,128)(2,1)}) %all-gather.5.cloned.1.call-update) | async-done | bytes 2097168 | tf_op jit(solution)/shard_map/all_gather | solution.py:15
  144.2 4.1 %fusion.8 = (f32[256]{0:T(256)S(1)}, f32[256,512]{1,0:T(8,128)S(1)}) fusion(bf16[256,4096]{1,0:T(8,128)(2,1)} %all-gather.5.cloned.1.call-done, bf16[4096,512]{1,0:T(8,128)(2,1)} %param.11), kind=kOutput, calls=%fused_computation.15 | convolution fusion | flops 1073872640 | bytes 6816768 | tf_op jit(solution)/shard_map/dot_general | solution.py:12
  148.3 39.4 %all-reduce.1 = (f32[256]{0:T(256)S(1)}, f32[1]{0:T(128)}) all-reduce(f32[256]{0:T(256)S(1)} %get-tuple-element.15, f32[1]{0:T(128)} %bitcast), channel_id=1, replica_groups=mesh['vocab'=16,'pipe'=2] {'vocab'}, use_global_device_ids=true, to_apply=%region_9.10 | all-reduce | flops 257 | bytes 2056 | tf_op jit(solution)/shard_map/pmax | solution.py:25
  187.8 0.2 fusion
  188.0 36.6 %all-reduce = (f32[256]{0:T(256)S(1)}, f32[256]{0:T(256)S(1)}, f32[256]{0:T(256)S(1)}) all-reduce(f32[256]{0:T(256)S(1)} %get-tuple-element.5, f32[256]{0:T(256)S(1)} %get-tuple-element.6, f32[256]{0:T(256)S(1)} %fusion), channel_id=1, replica_groups=mesh['vocab'=16,'pipe'=2] {'vocab'}, use_global_device_ids=true, to_apply=%region_5.6 | all-reduce | flops 768 | bytes 6144 | tf_op jit(solution)/shard_map/psum | solution.py:24
  224.6 0.0 copy-done
  224.6 0.0 copy-done.1
  224.6 5.5 %fusion.1 = f32[256,4096]{1,0:T(8,128)} fusion(bf16[4096,512]{1,0:T(8,128)(2,1)} %param.11, f32[256,512]{1,0:T(8,128)S(1)} %get-tuple-element.16, f32[256]{0:T(256)S(1)} %copy-done, f32[256]{0:T(256)S(1)} %get-tuple-element.9, f32[256]{0:T(256)S(1)} %get-tuple-element.10, s32[512]{0:T(512)S(1)} %iota_add_fusion, s32[256]{0:T(256)S(1)} %copy-done.1), kind=kOutput, calls=%fused_computation.6 | convolution fusion | flops 1074659328 | bytes 8919040 | tf_op jit(solution)/shard_map/dot_general | solution.py:33
  230.1 0.0 reduce-scatter.2.cloned.1.call-update
  230.8 0.6 add_subtract_fusion
  231.3 91.9 %reduce-scatter.2.cloned.1.call-done = f32[256,256]{1,0:T(8,128)} async-done(((f32[256,4096]{1,0:T(8,128)}), f32[256,256]{1,0:T(8,128)}) %reduce-scatter.2.cloned.1.call-update) | async-done | bytes 262160 | tf_op jit(solution)/shard_map/reduce_scatter | solution.py:36
  323.3 1.6 convert_element_type.15
  (1 shorter events, 0.0 us)
Async XLA Ops:
  7.2 114.0 %copy-start.2 = (s32[256]{0:T(256)S(1)}, s32[256]{0:T(256)}, u32[]{:S(2)}) copy-start(s32[256]{0:T(256)} %param.7) | copy-start | bytes 3076
  7.2 71.0 %all-gather.3.cloned.1.call-start = ((), (), s32[]{:S(2)}) async-start(), calls=%async_computation.1 | async-start | bytes 2228224 | tf_op jit(solution)/shard_map/all_gather | solution.py:14
  7.9 136.3 %all-gather.5.cloned.1.call-start = ((), (), s32[]{:S(2)}) async-start(), calls=%async_computation.2 | async-start | bytes 2228224 | tf_op jit(solution)/shard_map/all_gather | solution.py:15
  8.7 314.6 %reduce-scatter.2.cloned.1.call-start = ((), (), s32[]{:S(2)}) async-start(), calls=%async_computation.3 | async-start | bytes 4456448 | tf_op jit(solution)/shard_map/reduce_scatter | solution.py:36
  122.7 101.9 %copy-start = (f32[256]{0:T(256)S(1)}, f32[256]{0:T(256)}, u32[]{:S(2)}) copy-start(f32[256]{0:T(256)} %param.10) | copy-start | bytes 3076
  122.7 101.9 %copy-start.1 = (s32[256]{0:T(256)S(1)}, s32[256]{0:T(256)}, u32[]{:S(2)}) copy-start(s32[256]{0:T(256)} %param.9) | copy-start | bytes 3076
Sparse Core Ops, SparseCore 0:
  10.7 67.4 all-gather.2
  80.9 63.2 all-gather.4
  230.2 93.0 reduce-scatter.1
where the time goes:
time: 333 us
  waiting for transfers between devices  184 us (55%)
  blocking collectives  115 us (35%)
  between operations  15.6 us (5%)
  matrix products  13.8 us (4%)
  other arithmetic  3.94 us (1%)
    reduce_scatter x1, waiting for transfers between devices, shards(): lax.psum_scatter(grad_terms, 'vocab', scatter_dimension=1, tiled=True)  91.9 us
    all_gather x1, waiting for transfers between devices, shards(): scores_a = accumulate(lax.all_gather(hidden_a, 'vocab', axis=1, tiled=True))  69.5 us
    pmax x1, blocking collectives, shards(): peak_b = lax.pmax(row_peak_b, 'vocab')  39.4 us
    pmax x1, blocking collectives, shards(): peak_a, largest = lax.pmax((row_peak_a, abs_peak), 'vocab')  38.8 us
    psum x1, blocking collectives, shards(): total_a, label_a = lax.psum((own_total_a, label_local), 'vocab')  36.6 us
    all_gather x1, waiting for transfers between devices, shards(): scores_b = accumulate(lax.all_gather(hidden_b, 'vocab', axis=1, tiled=True))  21.5 us
    dot_general x2, matrix products, accumulate(): return jnp.dot(portion, out_weight, preferred_element_type=jnp.float32)  8.29 us
  transfers between devices with their start and end apart: 3, of which 3 were waited for; matrix products, arithmetic and copies ran while one was open for 2% of the time, Pallas kernels for 0%

commit v1 on v0

v1 whole, which is shorter than its diff:
```python
import functools

import jax
import jax.numpy as jnp
from jax import lax
from jax.experimental import pallas as pl
from jax.experimental.pallas import tpu as pltpu
from jax.sharding import PartitionSpec as P

MESH = pl.DeviceIdType.MESH
F32 = jnp.float32
BF16 = jnp.bfloat16
QUAD = 4
LANES = 128


def to_column(row):
    return jnp.broadcast_to(row, (LANES, row.shape[1])).T[:, :1]


def to_row(column):
    return jnp.broadcast_to(column, (column.shape[0], LANES)).T[:1, :]


def kernel(
    n, ha, la, hb, lb, cot, w_hbm, logits, loss, amax, grad,
    w, ga, gb, sa, sb, dl, send, near, x1, y1, x2, y2, r3, st_a, st_b, send_sem, recv_sem, w_sem,
):
    levels = n // QUAD
    tok, width = ha.shape
    half = tok // 2
    vocab = w.shape[1]
    me = lax.axis_index("vocab")
    z, q = me // QUAD, me % QUAD
    xq = (q // 2) * 2 + 1 - q % 2
    yq = (q + 2) % QUAD
    dq = QUAD - 1 - q
    xn, yn = z * QUAD + xq, z * QUAD + yq

    w_copy = pltpu.make_async_copy(w_hbm, w, w_sem)
    w_copy.start()
    barrier = pltpu.get_barrier_semaphore()
    for off in range(1, n):
        pl.semaphore_signal(
            barrier, inc=1, device_id={"vocab": lax.rem(me + off, n)}, device_id_type=MESH
        )

    def cols(index):
        return pl.ds(pl.multiple_of(index * width, width), width)

    gb[:, cols(me)] = hb[...]
    ga[:, cols(me)] = ha[...]
    pl.semaphore_wait(barrier, n - 1)

    copies = []

    def start(src, dst, to):
        k = len(copies)
        copy = pltpu.make_async_remote_copy(
            src_ref=src, dst_ref=dst, send_sem=send_sem.at[k], recv_sem=recv_sem.at[k],
            device_id={"vocab": to}, device_id_type=MESH,
        )
        copy.start()
        copies.append(copy)
        return copy

    def level(dz):
        return lax.rem(z + levels - dz, levels)

    class Gather:
        def __init__(self, own, whole):
            self.own, self.whole = own, whole
            self.z, self.x, self.y, self.dx, self.dy = {}, {}, {}, {}, {}

        def line(self):
            for dz in seq[1:]:
                to = lax.rem(z + dz, levels) * QUAD + q
                self.z[dz] = start(self.own, self.whole.at[:, cols(me)], to)

        def plane(self, dz):
            if dz:
                self.z[dz].wait_recv()
            block = self.whole.at[:, cols(level(dz) * QUAD + q)]
            src = block if dz else self.own
            self.x[dz] = start(src, block, xn)
            self.y[dz] = start(src, block, yn)

        def relay(self, dz):
            self.x[dz].wait_recv()
            block = self.whole.at[pl.ds(0, half), cols(level(dz) * QUAD + xq)]
            self.dx[dz] = start(block, block, yn)
            self.y[dz].wait_recv()
            block = self.whole.at[pl.ds(half, half), cols(level(dz) * QUAD + yq)]
            self.dy[dz] = start(block, block, xn)

        def multiply(self, dz, scores, first):
            self.dx[dz].wait_recv()
            self.dy[dz].wait_recv()
            depth = QUAD * width
            rows = pl.ds(pl.multiple_of(level(dz) * depth, depth), depth)
            term = jnp.dot(self.whole[:, rows], w[rows, :], preferred_element_type=F32)
            scores[...] = term if first else scores[...] + term

    def spread(stats):
        return [start(stats.at[me], stats.at[me], lax.rem(me + off, n)) for off in range(1, n)]

    seq = [0] + sorted(range(1, levels), key=lambda dz: min(dz, levels - dz))
    last = seq[-1]
    b, a = Gather(hb, gb), Gather(ha, ga)
    b.line()
    b.plane(0)
    for i in range(1, levels):
        b.plane(seq[i])
        b.relay(seq[i - 1])
        if i == 1:
            w_copy.wait()
        else:
            b.multiply(seq[i - 2], sb, i == 2)
    a.line()
    b.relay(last)
    a.plane(0)
    if levels > 1:
        b.multiply(seq[-2], sb, levels == 2)
    b.multiply(last, sb, levels == 1)

    scores = sb[...]
    peak = jnp.max(scores, axis=1, keepdims=True)
    total = jnp.sum(jnp.exp(scores - peak), axis=1, keepdims=True)
    st_b[me, :, pl.ds(0, tok)] = to_row(peak)
    st_b[me, :, pl.ds(tok, tok)] = to_row(total)
    stats_b = spread(st_b)

    held = max(1, levels - 1)
    for i in range(1, held):
        a.plane(seq[i])
        if i < held - 1:
            a.relay(seq[i - 1])
        else:
            a.relay(seq[i - 1])

    for copy in stats_b:
        copy.wait_recv()
    peaks, totals = st_b[:, :, pl.ds(0, tok)], st_b[:, :, pl.ds(tok, tok)]
    peak = jnp.max(peaks, axis=0)
    total = jnp.sum(totals * jnp.exp(peaks - peak[None]), axis=0)
    peak_c, inv_c, cot_c = to_column(peak), to_column(1.0 / total), to_column(cot[...])
    columns = me * vocab + lax.broadcasted_iota(jnp.int32, (tok, vocab), 1)
    probs = jnp.exp(sb[...] - peak_c) * inv_c
    onehot = (columns == to_column(lb[...])).astype(F32)
    dl[...] = ((probs - onehot) * cot_c).astype(BF16)

    def term(index):
        rows = pl.ds(pl.multiple_of(index * width, width), width)
        return lax.dot_general(
            dl[...], w[rows, :], (((1,), (1,)), ((), ())), preferred_element_type=F32
        )

    out = [dz for dz in seq if dz] + [0]
    cx, cy = {}, {}
    for dz in out:
        slot = send.at[3 * dz]
        slot[...] = term(level(dz) * QUAD + dq).astype(BF16)
        cx[dz] = start(slot.at[pl.ds(0, half)], x1.at[dz], xn)
        cy[dz] = start(slot.at[pl.ds(half, half)], y1.at[dz], yn)
    if held >= 2:
        a.relay(seq[held - 1])
    for i in range(held, levels):
        a.plane(seq[i])
    bx, by = {}, {}
    for dz in out:
        to_x, to_y = send.at[3 * dz + 1], send.at[3 * dz + 2]
        tx = term(level(dz) * QUAD + xq)
        ty = term(level(dz) * QUAD + yq)
        cx[dz].wait_recv()
        cy[dz].wait_recv()
        to_x[pl.ds(0, half), :] = tx[:half].astype(BF16)
        to_x[pl.ds(half, half), :] = (tx[half:] + y1[dz].astype(F32)).astype(BF16)
        to_y[pl.ds(0, half), :] = (ty[:half] + x1[dz].astype(F32)).astype(BF16)
        to_y[pl.ds(half, half), :] = ty[half:].astype(BF16)
        bx[dz] = start(to_x, x2.at[dz], xn)
        by[dz] = start(to_y, y2.at[dz], yn)
    for i in range(held, levels):
        a.relay(seq[i])

    for i in range(levels):
        a.multiply(seq[i], sa, i == 0)
    scores = sa[...]
    logits[...] = scores.astype(BF16)
    peak = jnp.max(scores, axis=1, keepdims=True)
    total = jnp.sum(jnp.exp(scores - peak), axis=1, keepdims=True)
    label = jnp.sum(
        jnp.where(columns == to_column(la[...]), scores, 0.0), axis=1, keepdims=True
    )
    largest = jnp.max(jnp.abs(scores), axis=1, keepdims=True)
    for i, value in enumerate((peak, total, label, largest)):
        st_a[me, :, pl.ds(i * tok, tok)] = to_row(value)
    stats_a = spread(st_a)

    lines = {}
    for dz in out:
        near[...] = term(level(dz) * QUAD + q)
        bx[dz].wait_recv()
        by[dz].wait_recv()
        sums = near[...] + x2[dz].astype(F32) + y2[dz].astype(F32)
        if dz:
            slot = send.at[3 * levels + dz - 1]
            slot[...] = sums.astype(BF16)
            lines[dz] = start(slot, r3.at[dz - 1], level(dz) * QUAD + q)
        else:
            near[...] = sums

    for copy in stats_a:
        copy.wait_recv()
    peaks, totals = st_a[:, :, pl.ds(0, tok)], st_a[:, :, pl.ds(tok, tok)]
    peak = jnp.max(peaks, axis=0)
    total = jnp.sum(totals * jnp.exp(peaks - peak[None]), axis=0)
    label = jnp.sum(st_a[:, :, pl.ds(2 * tok, tok)], axis=0)
    loss[...] = jnp.log(total) + peak - label
    largest = jnp.max(jnp.max(st_a[:, :, pl.ds(3 * tok, tok)], axis=0), axis=1, keepdims=True)
    amax[...] = 448.0 / largest

    sums = near[...]
    for dz in out[:-1]:
        lines[dz].wait_recv()
        sums = sums + r3[dz - 1].astype(F32)
    grad[...] = sums.astype(BF16)
    for copy in copies:
        copy.wait_send()


def fused(n, hidden_a, labels_a, hidden_b, labels_b, loss_cotangent, out_weight):
    tok, width = hidden_a.shape
    depth, vocab = out_weight.shape
    levels = n // QUAD
    half = tok // 2
    sends = 3 * (5 * levels - 1) + 2 * (n - 1)
    vmem = pl.BlockSpec(memory_space=pltpu.VMEM)
    row = lambda value: value.reshape(1, tok)
    logits, loss, amax, grad = pl.pallas_call(
        functools.partial(kernel, n),
        out_shape=(
            jax.ShapeDtypeStruct((tok, vocab), BF16),
            jax.ShapeDtypeStruct((1, tok), F32),
            jax.ShapeDtypeStruct((1, 1), F32),
            jax.ShapeDtypeStruct((tok, width), BF16),
        ),
        in_specs=[vmem] * 5 + [pl.BlockSpec(memory_space=pl.ANY)],
        out_specs=(vmem,) * 4,
        scratch_shapes=[
            pltpu.VMEM((depth, vocab), BF16),
            pltpu.VMEM((tok, depth), BF16),
            pltpu.VMEM((tok, depth), BF16),
            pltpu.VMEM((tok, vocab), F32),
            pltpu.VMEM((tok, vocab), F32),
            pltpu.VMEM((tok, vocab), BF16),
            pltpu.VMEM((4 * levels - 1, tok, width), BF16),
            pltpu.VMEM((tok, width), F32),
            pltpu.VMEM((levels, half, width), BF16),
            pltpu.VMEM((levels, half, width), BF16),
            pltpu.VMEM((levels, tok, width), BF16),
            pltpu.VMEM((levels, tok, width), BF16),
            pltpu.VMEM((max(1, levels - 1), tok, width), BF16),
            pltpu.VMEM((n, 1, 4 * tok), F32),
            pltpu.VMEM((n, 1, 2 * tok), F32),
            pltpu.SemaphoreType.DMA((sends,)),
            pltpu.SemaphoreType.DMA((sends,)),
            pltpu.SemaphoreType.DMA,
        ],
        compiler_params=pltpu.CompilerParams(
            collective_id=0, has_side_effects=True, vmem_limit_bytes=48 * 1024 * 1024
        ),
    )(hidden_a, row(labels_a), hidden_b, row(labels_b), row(loss_cotangent), out_weight)
    return logits, loss.reshape(tok), amax.reshape(1), grad


def plain(n, hidden_a, labels_a, hidden_b, labels_b, loss_cotangent, out_weight):
    offset = lax.axis_index("vocab") * out_weight.shape[1]

    def accumulate(portion):
        return jnp.dot(portion, out_weight, preferred_element_type=jnp.float32)

    scores_a = accumulate(lax.all_gather(hidden_a, "vocab", axis=1, tiled=True))
    scores_b = accumulate(lax.all_gather(hidden_b, "vocab", axis=1, tiled=True))
    columns_a = offset + lax.broadcasted_iota(jnp.int32, scores_a.shape, 1)
    columns_b = offset + lax.broadcasted_iota(jnp.int32, scores_b.shape, 1)
    label_local = jnp.sum(jnp.where(columns_a == labels_a[:, None], scores_a, 0.0), axis=1)
    abs_peak = jnp.max(jnp.abs(scores_a)).reshape(1)
    peak_a, largest = lax.pmax((jnp.max(scores_a, axis=1), abs_peak), "vocab")
    own_total_a = jnp.sum(jnp.exp(scores_a - peak_a[:, None]), axis=1)
    total_a, label_a = lax.psum((own_total_a, label_local), "vocab")
    peak_b = lax.pmax(jnp.max(scores_b, axis=1), "vocab")
    exps_b = jnp.exp(scores_b - peak_b[:, None])
    total_b = lax.psum(jnp.sum(exps_b, axis=1), "vocab")
    onehot = (columns_b == labels_b[:, None]).astype(jnp.float32)
    dlogits_b = ((exps_b / total_b[:, None] - onehot) * loss_cotangent[:, None]).astype(BF16)
    grad_terms = lax.dot_general(
        dlogits_b, out_weight, (((1,), (1,)), ((), ())), preferred_element_type=jnp.float32
    )
    grad = lax.psum_scatter(grad_terms, "vocab", scatter_dimension=1, tiled=True).astype(BF16)
    return scores_a.astype(BF16), jnp.log(total_a) + peak_a - label_a, 448.0 / largest, grad


def shards(n, hidden_a, *rest):
    aligned = hidden_a.shape[0] % (2 * LANES) == 0 and hidden_a.shape[1] % LANES == 0
    form = fused if n % QUAD == 0 and aligned else plain
    return form(n, hidden_a, *rest)


def solution(mesh):
    return jax.shard_map(
        functools.partial(shards, mesh.shape["vocab"]),
        mesh=mesh,
        in_specs=(
            P("pipe", "vocab"),
            P("pipe"),
            P("pipe", "vocab"),
            P("pipe"),
            P("pipe"),
            P("pipe", "vocab"),
        ),
        out_specs=(P("pipe", "vocab"), P("pipe"), P("pipe"), P("pipe", "vocab")),
        check_vma=False,
    )
```

time: 333 us -> 86.6 us (0.26)
  waiting for transfers between devices: 184 us -> 0 us
  blocking collectives: 115 us -> 0 us
  Pallas kernels: 0 us -> 75.9 us
  matrix products: 13.8 us -> 0 us
  between operations: 15.6 us -> 2.48 us
  local copies, waits for them, and re-layouts: 0.01 us -> 7.95 us
  other arithmetic: 3.94 us -> 0 us
    reduce_scatter x1 -> x0, waiting for transfers between devices: 91.9 us -> none  [shards(): lax.psum_scatter(grad_terms, 'vocab', scatter_dimension=1, tiled=True)]
    all_gather x2 -> x0, waiting for transfers between devices: 91 us -> none  [the longest x1 69.5 us: shards(): scores_a = accumulate(lax.all_gather(hidden_a, 'vocab', axis=1, tiled=True))]
    pmax x2 -> x0, blocking collectives: 78.2 us -> none  [the longest x1 39.4 us: shards(): peak_b = lax.pmax(row_peak_b, 'vocab')]
    pallas_call x0 -> x1, Pallas kernels: none -> 75.9 us  [fused(): pl.pallas_call(functools.partial(kernel, n), out_shape=(jax.ShapeDtypeStr...]
    psum x1 -> x0, blocking collectives: 36.6 us -> none  [shards(): total_a, label_a = lax.psum((own_total_a, label_local), 'vocab')]
    dot_general x3 -> x0, matrix products: 13.8 us -> none  [the longest x2 8.29 us: accumulate(): return jnp.dot(portion, out_weight, preferred_element_type=jnp.float32)]
    unnamed x6 -> x15, local copies, waits for them, and re-layouts: 0.01 us -> 7.95 us
  transfers between devices with their start and end apart: 3 -> 0, of which waited for: 3 -> 0; matrix products, arithmetic and copies ran while one was open for 2% -> 0% of each run, Pallas kernels for 0% -> 0%
where the time goes in v1:
time: 86.6 us; the launch traced here: 86.3 us
  Pallas kernels  75.9 us (88%)
  local copies, waits for them, and re-layouts  7.95 us (9%)
  between operations  2.48 us (3%)
    pallas_call x1, Pallas kernels, fused(): pl.pallas_call(functools.partial(kernel, n), out_shape=(jax.ShapeDtypeStr...  75.9 us
    unnamed x15, local copies, waits for them, and re-layouts  7.95 us

profile of v1, /device:TPU:0, one launch (start us, length us, event | category | flops | bytes accessed | tf_op | source)
XLA Modules:
  0.0 86.3 jit_solution(12349821936324951411)
XLA Ops:
  0.6 0.0 copy-start
  0.6 2.2 %copy-done = bf16[4096,512]{1,0:T(8,128)(2,1)S(1)} copy-done((bf16[4096,512]{1,0:T(8,128)(2,1)S(1)}, bf16[4096,512]{1,0:T(8,128)(2,1)}, u32[]{:S(2)}) %copy-start) | copy-done | bytes 4194328
  2.8 0.0 copy-start.1
  2.8 0.9 %copy-done.1 = bf16[256,256]{1,0:T(8,128)(2,1)S(1)} copy-done((bf16[256,256]{1,0:T(8,128)(2,1)S(1)}, bf16[256,256]{1,0:T(8,128)(2,1)}, u32[]{:S(2)}) %copy-start.1) | copy-done | bytes 131096
  3.7 0.0 copy-start.2
  3.7 0.9 %copy-done.2 = bf16[256,256]{1,0:T(8,128)(2,1)S(1)} copy-done((bf16[256,256]{1,0:T(8,128)(2,1)S(1)}, bf16[256,256]{1,0:T(8,128)(2,1)}, u32[]{:S(2)}) %copy-start.2) | copy-done | bytes 131096
  4.6 0.0 copy-start.3
  4.6 0.7 copy-done.3
  5.3 0.0 copy-start.4
  5.3 0.7 copy-done.4
  6.0 0.0 copy-start.5
  6.0 0.7 copy-done.5
  6.7 75.9 %shard_map.93 = (bf16[256,512]{1,0:T(8,128)(2,1)S(1)}, f32[1,256]{1,0:T(1,128)S(1)}, f32[1,1]{1,0:T(1,128)}, bf16[256,256]{1,0:T(8,128)(2,1)S(1)}) custom-call(bf16[256,256]{1,0:T(8,128)(2,1)S(1)} %copy-done.1, s32[1,256]{1,0:T(1,128)S(1)} %bitcast.5, bf16[256,256]{1,0:T(8,128)(2,1)S(1)} %copy-done.2, s32[1,256]{1,0:T(1,128)S(1)} %bitcast.6, ...), custom_call_target="tpu_custom_call" | custom-call | tf_op jit(solution)/shard_map/pallas_call | solution.py:239
  82.5 0.7 copy.14
  83.2 0.6 copy.15
  84.5 0.7 copy.17
Async XLA Ops:
  0.6 2.2 %copy-start = (bf16[4096,512]{1,0:T(8,128)(2,1)S(1)}, bf16[4096,512]{1,0:T(8,128)(2,1)}, u32[]{:S(2)}) copy-start(bf16[4096,512]{1,0:T(8,128)(2,1)} %w_hbm.1) | copy-start | bytes 12582916
  2.8 0.9 %copy-start.1 = (bf16[256,256]{1,0:T(8,128)(2,1)S(1)}, bf16[256,256]{1,0:T(8,128)(2,1)}, u32[]{:S(2)}) copy-start(bf16[256,256]{1,0:T(8,128)(2,1)} %ha.1) | copy-start | bytes 393220
  3.7 0.9 %copy-start.2 = (bf16[256,256]{1,0:T(8,128)(2,1)S(1)}, bf16[256,256]{1,0:T(8,128)(2,1)}, u32[]{:S(2)}) copy-start(bf16[256,256]{1,0:T(8,128)(2,1)} %hb.1) | copy-start | bytes 393220
  4.6 0.7 copy-start.3
  5.3 0.7 copy-start.4
  6.0 0.7 copy-start.5

commit v2 on v1

--- a/solution.py
+++ b/solution.py
@@ -22,9 +22,17 @@
     return jnp.broadcast_to(column, (column.shape[0], LANES)).T[:1, :]
 
 
+def flip(index, mask):
+    bit, out = 1, 0
+    while bit <= mask:
+        out = out + lax.rem(index // bit + (mask // bit) % 2, 2) * bit
+        bit *= 2
+    return out + (index // bit) * bit
+
+
 def kernel(
-    n, ha, la, hb, lb, cot, w_hbm, logits, loss, amax, grad,
-    w, ga, gb, sa, sb, dl, send, near, x1, y1, x2, y2, r3, st_a, st_b, send_sem, recv_sem, w_sem,
+    n, ha_hbm, la_hbm, hb_hbm, lb_hbm, cot_hbm, w_hbm, logits, loss, amax, grad,
+    ha, la, hb, lb, cot, w, ga, gb, sa, sb, dl, send, near, x1, y1, x2, y2, r3, st_a, st_b, send_sem, recv_sem, load_sem,
 ):
     levels = n // QUAD
     tok, width = ha.shape
@@ -37,20 +45,23 @@
     dq = QUAD - 1 - q
     xn, yn = z * QUAD + xq, z * QUAD + yq
 
-    w_copy = pltpu.make_async_copy(w_hbm, w, w_sem)
-    w_copy.start()
     barrier = pltpu.get_barrier_semaphore()
-    for off in range(1, n):
-        pl.semaphore_signal(
-            barrier, inc=1, device_id={"vocab": lax.rem(me + off, n)}, device_id_type=MESH
-        )
+    peers = [flip(z, k) * QUAD + q for k in range(1, levels)] + [xn, yn]
+    for peer in peers:
+        pl.semaphore_signal(barrier, inc=1, device_id={"vocab": peer}, device_id_type=MESH)
+    pairs = ((hb_hbm, hb), (ha_hbm, ha), (la_hbm, la), (lb_hbm, lb), (cot_hbm, cot), (w_hbm, w))
+    loads = [
+        pltpu.make_async_copy(src, dst, load_sem.at[i]) for i, (src, dst) in enumerate(pairs)
+    ]
+    for load in loads:
+        load.start()
 
     def cols(index):
         return pl.ds(pl.multiple_of(index * width, width), width)
 
-    gb[:, cols(me)] = hb[...]
-    ga[:, cols(me)] = ha[...]
-    pl.semaphore_wait(barrier, n - 1)
+    loads[0].wait()
+    loads[1].wait()
+    pl.semaphore_wait(barrier, len(peers))
 
     copies = []
 
@@ -65,37 +76,47 @@
         return copy
 
     def level(dz):
-        return lax.rem(z + levels - dz, levels)
+        return flip(z, dz)
 
     class Gather:
-        def __init__(self, own, whole):
-            self.own, self.whole = own, whole
+        def __init__(self, own, whole, first, count):
+            self.own, self.whole = own.at[pl.ds(first, count)], whole
+            self.all, self.front = pl.ds(first, count), pl.ds(first, count // 2)
+            self.back = pl.ds(first + count // 2, count // 2)
             self.z, self.x, self.y, self.dx, self.dy = {}, {}, {}, {}, {}
 
         def line(self):
             for dz in seq[1:]:
-                to = lax.rem(z + dz, levels) * QUAD + q
-                self.z[dz] = start(self.own, self.whole.at[:, cols(me)], to)
+                to = flip(z, dz) * QUAD + q
+                self.z[dz] = start(self.own, self.whole.at[self.all, cols(me)], to)
 
         def plane(self, dz):
-            if dz:
+            if dz and self.z:
                 self.z[dz].wait_recv()
-            block = self.whole.at[:, cols(level(dz) * QUAD + q)]
+            block = self.whole.at[self.all, cols(level(dz) * QUAD + q)]
             src = block if dz else self.own
             self.x[dz] = start(src, block, xn)
             self.y[dz] = start(src, block, yn)
 
         def relay(self, dz):
             self.x[dz].wait_recv()
-            block = self.whole.at[pl.ds(0, half), cols(level(dz) * QUAD + xq)]
+            block = self.whole.at[self.front, cols(level(dz) * QUAD + xq)]
             self.dx[dz] = start(block, block, yn)
             self.y[dz].wait_recv()
-            block = self.whole.at[pl.ds(half, half), cols(level(dz) * QUAD + yq)]
+            block = self.whole.at[self.back, cols(level(dz) * QUAD + yq)]
             self.dy[dz] = start(block, block, xn)
 
-        def multiply(self, dz, scores, first):
+        def corner(self, dz):
             self.dx[dz].wait_recv()
             self.dy[dz].wait_recv()
+
+        def lines(self, column):
+            block = self.whole.at[self.all, cols(z * QUAD + column)]
+            for dz in seq[1:]:
+                src = self.own if column is q else block
+                self.z[dz, len(self.z)] = start(src, block, flip(z, dz) * QUAD + q)
+
+        def multiply(self, dz, scores, first):
             depth = QUAD * width
             rows = pl.ds(pl.multiple_of(level(dz) * depth, depth), depth)
             term = jnp.dot(self.whole[:, rows], w[rows, :], preferred_element_type=F32)
@@ -104,24 +125,50 @@
     def spread(stats):
         return [start(stats.at[me], stats.at[me], lax.rem(me + off, n)) for off in range(1, n)]
 
-    seq = [0] + sorted(range(1, levels), key=lambda dz: min(dz, levels - dz))
+    seq = list(range(levels))
     last = seq[-1]
-    b, a = Gather(hb, gb), Gather(ha, ga)
+    b = Gather(hb, gb, 0, tok)
+    cut = tok * 7 // 8
+    a = Gather(ha, ga, 0, cut)
+    late = Gather(ha, ga, cut, tok - cut)
+    b.plane(0)
     b.line()
-    b.plane(0)
+    late.plane(0)
+    gb[:, cols(me)] = hb[...]
+    ga[:, cols(me)] = ha[...]
     for i in range(1, levels):
-        b.plane(seq[i])
-        b.relay(seq[i - 1])
+        b.plane(i)
+        b.relay(i - 1)
         if i == 1:
-            w_copy.wait()
+            late.relay(0)
+            for load in loads[2:]:
+                load.wait()
         else:
-            b.multiply(seq[i - 2], sb, i == 2)
-    a.line()
+            b.corner(i - 2)
+            b.multiply(i - 2, sb, i == 2)
+        if i == last:
+            a.line()
+            late.lines(q)
+            late.lines(xq)
+            late.lines(yq)
+            late.corner(0)
+            late.lines(dq)
     b.relay(last)
-    a.plane(0)
-    if levels > 1:
-        b.multiply(seq[-2], sb, levels == 2)
-    b.multiply(last, sb, levels == 1)
+
+    order = [functools.partial(a.plane, 0)]
+    for i in range(1, levels):
+        order += [functools.partial(a.plane, i), functools.partial(a.relay, i - 1)]
+    order.append(functools.partial(a.relay, last))
+
+    def advance(count):
+        for step in order[:count]:
+            step()
+        del order[:count]
+
+    advance(2)
+    for i in range(max(0, levels - 2), levels):
+        b.corner(i)
+        b.multiply(i, sb, i == 0)
 
     scores = sb[...]
     peak = jnp.max(scores, axis=1, keepdims=True)
@@ -130,14 +177,7 @@
     st_b[me, :, pl.ds(tok, tok)] = to_row(total)
     stats_b = spread(st_b)
 
-    held = max(1, levels - 1)
-    for i in range(1, held):
-        a.plane(seq[i])
-        if i < held - 1:
-            a.relay(seq[i - 1])
-        else:
-            a.relay(seq[i - 1])
-
+    advance(4)
     for copy in stats_b:
         copy.wait_recv()
     peaks, totals = st_b[:, :, pl.ds(0, tok)], st_b[:, :, pl.ds(tok, tok)]
@@ -155,17 +195,14 @@
             dl[...], w[rows, :], (((1,), (1,)), ((), ())), preferred_element_type=F32
         )
 
-    out = [dz for dz in seq if dz] + [0]
+    out = seq[::-1]
     cx, cy = {}, {}
     for dz in out:
         slot = send.at[3 * dz]
         slot[...] = term(level(dz) * QUAD + dq).astype(BF16)
         cx[dz] = start(slot.at[pl.ds(0, half)], x1.at[dz], xn)
         cy[dz] = start(slot.at[pl.ds(half, half)], y1.at[dz], yn)
-    if held >= 2:
-        a.relay(seq[held - 1])
-    for i in range(held, levels):
-        a.plane(seq[i])
+    advance(len(order))
     bx, by = {}, {}
     for dz in out:
         to_x, to_y = send.at[3 * dz + 1], send.at[3 * dz + 2]
@@ -179,25 +216,36 @@
         to_y[pl.ds(half, half), :] = ty[half:].astype(BF16)
         bx[dz] = start(to_x, x2.at[dz], xn)
         by[dz] = start(to_y, y2.at[dz], yn)
-    for i in range(held, levels):
-        a.relay(seq[i])
-
-    for i in range(levels):
-        a.multiply(seq[i], sa, i == 0)
-    scores = sa[...]
-    logits[...] = scores.astype(BF16)
-    peak = jnp.max(scores, axis=1, keepdims=True)
-    total = jnp.sum(jnp.exp(scores - peak), axis=1, keepdims=True)
-    label = jnp.sum(
-        jnp.where(columns == to_column(la[...]), scores, 0.0), axis=1, keepdims=True
-    )
-    largest = jnp.max(jnp.abs(scores), axis=1, keepdims=True)
-    for i, value in enumerate((peak, total, label, largest)):
-        st_a[me, :, pl.ds(i * tok, tok)] = to_row(value)
-    stats_a = spread(st_a)
+
+    def finish_a(step):
+        a.corner(step)
+        for key, copy in late.z.items():
+            if key[0] == step:
+                copy.wait_recv()
+        a.multiply(step, sa, step == 0)
 
     lines = {}
-    for dz in out:
+    seen = 0
+    for turn, dz in enumerate(out):
+        if turn == len(out) - 1:
+            for i in range(seen, levels):
+                finish_a(i)
+            scores = sa[...]
+            logits[...] = scores.astype(BF16)
+            peak = jnp.max(scores, axis=1, keepdims=True)
+            total = jnp.sum(jnp.exp(scores - peak), axis=1, keepdims=True)
+            label = jnp.sum(
+                jnp.where(columns == to_column(la[...]), scores, 0.0), axis=1, keepdims=True
+            )
+            largest = jnp.max(jnp.abs(scores), axis=1, keepdims=True)
+            for i, value in enumerate((peak, total, label, largest)):
+                st_a[me, :, pl.ds(i * tok, tok)] = to_row(value)
+            stats_a = spread(st_a)
+
+        elif turn:
+            for i in range(seen, min(seen + 2, levels)):
+                finish_a(i)
+            seen = min(seen + 2, levels)
         near[...] = term(level(dz) * QUAD + q)
         bx[dz].wait_recv()
         by[dz].wait_recv()
@@ -233,7 +281,7 @@
     depth, vocab = out_weight.shape
     levels = n // QUAD
     half = tok // 2
-    sends = 3 * (5 * levels - 1) + 2 * (n - 1)
+    sends = 3 * (5 * levels - 1) + 2 * (n - 1) + 4 + 4 * (levels - 1)
     vmem = pl.BlockSpec(memory_space=pltpu.VMEM)
     row = lambda value: value.reshape(1, tok)
     logits, loss, amax, grad = pl.pallas_call(
@@ -244,9 +292,14 @@
             jax.ShapeDtypeStruct((1, 1), F32),
             jax.ShapeDtypeStruct((tok, width), BF16),
         ),
-        in_specs=[vmem] * 5 + [pl.BlockSpec(memory_space=pl.ANY)],
+        in_specs=[pl.BlockSpec(memory_space=pltpu.HBM)] * 6,
         out_specs=(vmem,) * 4,
         scratch_shapes=[
+            pltpu.VMEM((tok, width), BF16),
+            pltpu.VMEM((1, tok), jnp.int32),
+            pltpu.VMEM((tok, width), BF16),
+            pltpu.VMEM((1, tok), jnp.int32),
+            pltpu.VMEM((1, tok), F32),
             pltpu.VMEM((depth, vocab), BF16),
             pltpu.VMEM((tok, depth), BF16),
             pltpu.VMEM((tok, depth), BF16),
@@ -264,10 +317,10 @@
             pltpu.VMEM((n, 1, 2 * tok), F32),
             pltpu.SemaphoreType.DMA((sends,)),
             pltpu.SemaphoreType.DMA((sends,)),
-            pltpu.SemaphoreType.DMA,
+            pltpu.SemaphoreType.DMA((6,)),
         ],
         compiler_params=pltpu.CompilerParams(
-            collective_id=0, has_side_effects=True, vmem_limit_bytes=48 * 1024 * 1024
+            collective_id=0, has_side_effects=True, vmem_limit_bytes=67_043_328
         ),
     )(hidden_a, row(labels_a), hidden_b, row(labels_b), row(loss_cotangent), out_weight)
     return logits, loss.reshape(tok), amax.reshape(1), grad
@@ -302,7 +355,9 @@
 
 def shards(n, hidden_a, *rest):
     aligned = hidden_a.shape[0] % (2 * LANES) == 0 and hidden_a.shape[1] % LANES == 0
-    form = fused if n % QUAD == 0 and aligned else plain
+    levels = n // QUAD
+    staged = n % QUAD == 0 and levels > 1 and levels & (levels - 1) == 0
+    form = fused if staged and aligned else plain
     return form(n, hidden_a, *rest)
 
 

time: 86.6 us -> 74 us (0.85)
  Pallas kernels: 75.9 us -> 66.9 us
  local copies, waits for them, and re-layouts: 7.95 us -> 4.43 us
    pallas_call x1, Pallas kernels: 75.9 us -> 66.9 us  [fused(): pl.pallas_call(functools.partial(kernel, n), out_shape=(jax.ShapeDtypeStr...]
    unnamed x15 -> x3, local copies, waits for them, and re-layouts: 7.95 us -> 4.43 us
where the time goes in v2:
time: 74 us; the launch traced here: 73.8 us
  Pallas kernels  66.9 us (90%)
  local copies, waits for them, and re-layouts  4.43 us (6%)
  between operations  2.47 us (3%)
    pallas_call x1, Pallas kernels, fused(): pl.pallas_call(functools.partial(kernel, n), out_shape=(jax.ShapeDtypeStr...  66.9 us
    unnamed x3, local copies, waits for them, and re-layouts  4.43 us

profile of v2, /device:TPU:0, one launch (start us, length us, event | category | flops | bytes accessed | tf_op | source)
XLA Modules:
  0.0 73.8 jit_solution(14539432769522490059)
XLA Ops:
  0.6 66.9 %shard_map.93 = (bf16[256,512]{1,0:T(8,128)(2,1)}, f32[1,256]{1,0:T(1,128)}, f32[1,1]{1,0:T(1,128)}, bf16[256,256]{1,0:T(8,128)(2,1)}) custom-call(bf16[256,256]{1,0:T(8,128)(2,1)} %ha_hbm.1, s32[1,256]{1,0:T(1,128)} %bitcast.5, bf16[256,256]{1,0:T(8,128)(2,1)} %hb_hbm.1, s32[1,256]{1,0:T(1,128)} %bitcast.6, f32[1,256]{1,0:T(1,128)} %bitcast.7, ...), custom_call_target="tpu_custom_call" | custom-call | tf_op jit(solution)/shard_map/pallas_call | solution.py:287
  67.5 1.7 %copy.14 = bf16[256,512]{1,0:T(8,128)(2,1)} copy(bf16[256,512]{1,0:T(8,128)(2,1)} %get-tuple-element.16) | data formatting | bytes 524288
  69.2 1.2 %copy.15 = f32[256]{0:T(256)} copy(f32[256]{0:T(256)} %bitcast.8) | data formatting | bytes 2048
  71.1 1.6 %copy.17 = bf16[256,256]{1,0:T(8,128)(2,1)} copy(bf16[256,256]{1,0:T(8,128)(2,1)} %get-tuple-element.19) | data formatting | bytes 262144
